TPU v7x, 32 devices: a whole 2x2x4 slice. The times are simulated.
32 devices in a mesh: row: 8 (over z, core), col: 4 (over y, x).
Axes of the slice: x: 2, y: 2, z: 4, core: 2. Of those that a mesh axis runs over, the one named last changes fastest.
Arguments:
- psi: bfloat16 [1024, 4096], P(('row', 'col')), may hold values from -6 to 6
- hpsi: bfloat16 [1024, 4096], P(('row', 'col')), may hold values from -0.1875 to 0.1875
- eigvec: bfloat16 [4, 8, 128, 8, 4, 128], P(None, 'row', None, None, 'col'), may hold values from -0.09375 to 0.09375
Outputs:
- correlation_tiles: float32 [4, 8, 128, 8, 4, 128], P(None, 'row', None, None, 'col')
- updated_tiles: float32 [4, 8, 128, 8, 4, 128], P(None, 'row', None, None, 'col')
- diag_part: float32 [16], replicated
- offdiag_part: float32 [16], replicated
- rotated: bfloat16 [1024, 8, 4, 128], P('row', None, 'col')
All inputs are finite; a program needn't handle non-finite values.
Results may differ from a plain program's by a relative error of at most 0.001.
Values may be sent and summed in bfloat16 or wider, within the bound.
A program may use at most 128 MiB of HBM per device.

v0:
```python
import jax
import jax.numpy as jnp
from jax import lax
from jax.sharding import PartitionSpec as P

PB = 16


def broadcast(array, axis, root):
    mine = lax.axis_index(axis) == root
    return lax.psum(jnp.where(mine, array, jnp.zeros_like(array)), axis)


def inner(left, right):
    return lax.dot_general(
        left, right, (((0,), (0,)), ((), ())), preferred_element_type=jnp.float32
    )


def on_device(psi, hpsi, eigvec):
    highest = lax.Precision.HIGHEST
    g_rows = psi.shape[0]
    bands = psi.shape[1]
    row_tiles = eigvec.shape[0]
    tile_size = eigvec.shape[2]
    col_tiles = eigvec.shape[3]
    row_count = lax.axis_size("row")
    col_count = lax.axis_size("col")
    row_id = lax.axis_index("row")
    col_id = lax.axis_index("col")
    gvecs = g_rows * row_count * col_count
    row_width = row_tiles * tile_size
    col_width = col_tiles * tile_size
    lifted = (
        psi.reshape(1, g_rows, row_tiles, row_count, tile_size),
        hpsi.reshape(1, g_rows, row_tiles, row_count, tile_size),
    )
    swapped = (
        lax.all_to_all(lifted[0], "row", split_axis=3, concat_axis=0, tiled=True),
        lax.all_to_all(lifted[1], "row", split_axis=3, concat_axis=0, tiled=True),
    )
    joined = (
        lax.all_gather(swapped[0], "col", axis=1, tiled=True),
        lax.all_gather(swapped[1], "col", axis=1, tiled=True),
    )
    psi_rows = joined[0].reshape(gvecs, row_width)
    hpsi_rows = joined[1].reshape(gvecs, row_width)
    lowered = (
        psi.reshape(g_rows, col_tiles, col_count, tile_size),
        hpsi.reshape(g_rows, col_tiles, col_count, tile_size),
    )
    moved = (
        lax.all_to_all(lowered[0], "col", split_axis=2, concat_axis=0, tiled=True),
        lax.all_to_all(lowered[1], "col", split_axis=2, concat_axis=0, tiled=True),
    )
    stacked = (
        lax.all_gather(moved[0], "row", axis=0, tiled=True),
        lax.all_gather(moved[1], "row", axis=0, tiled=True),
    )
    psi_cols = stacked[0].reshape(gvecs, col_width)
    hpsi_cols = stacked[1].reshape(gvecs, col_width)
    reduced = 0.5 * (inner(psi_rows, hpsi_cols) + inner(hpsi_rows, psi_cols))
    correlation = inner(psi_rows, psi_cols) / float(gvecs)
    blocks = reduced.reshape(row_tiles, tile_size, col_tiles, tile_size)
    leading = blocks[:, :, 0, :PB]
    shared = broadcast(leading, "col", 0)
    panel = lax.all_gather(
        shared.reshape(row_tiles, 1, tile_size, PB), "row", axis=1, tiled=True
    ).reshape(bands, PB)

    def product(vector):
        local_vec = lax.dynamic_index_in_dim(
            vector.reshape(col_tiles, col_count, tile_size), col_id, 1, keepdims=False
        )
        partial_sum = jnp.einsum("atbs,bs->at", blocks, local_vec, precision=highest)
        summed = lax.psum(partial_sum, "col")
        result = lax.all_gather(
            summed.reshape(row_tiles, 1, tile_size), "row", axis=1, tiled=True
        ).reshape(bands)
        return result

    positions = jnp.arange(bands)
    slots = jnp.arange(PB)

    def reflect(step, carry):
        vecs, images, diagonal, offdiag = carry
        column = lax.dynamic_index_in_dim(panel, step, 1, keepdims=False)
        head_v = lax.dynamic_index_in_dim(vecs, step, 0, keepdims=False)
        head_w = lax.dynamic_index_in_dim(images, step, 0, keepdims=False)
        column = (
            column
            - jnp.dot(vecs, head_w, precision=highest)
            - jnp.dot(images, head_v, precision=highest)
        )
        pivot = lax.dynamic_index_in_dim(column, step + 1, 0, keepdims=False)
        below = positions > step + 1
        tail = jnp.sum(jnp.where(below, column * column, 0.0))
        length = jnp.sqrt(pivot * pivot + tail)
        beta = jnp.where(pivot >= 0.0, -length, length)
        tau = (beta - pivot) / beta
        vector = jnp.where(
            positions == step + 1, 1.0, jnp.where(below, column / (pivot - beta), 0.0)
        )
        image = product(vector)
        image = image - jnp.dot(vecs, jnp.dot(vector, images, precision=highest), precision=highest)
        image = image - jnp.dot(images, jnp.dot(vector, vecs, precision=highest), precision=highest)
        image = tau * image
        image = image - 0.5 * tau * jnp.dot(image, vector, precision=highest) * vector
        pick = slots == step
        vecs = jnp.where(pick[None, :], vector[:, None], vecs)
        images = jnp.where(pick[None, :], image[:, None], images)
        diagonal = jnp.where(
            pick, lax.dynamic_index_in_dim(column, step, 0, keepdims=False), diagonal
        )
        offdiag = jnp.where(pick, beta, offdiag)
        return (vecs, images, diagonal, offdiag)

    start_state = (
        jnp.zeros((bands, PB), jnp.float32),
        jnp.zeros((bands, PB), jnp.float32),
        jnp.zeros((PB,), jnp.float32),
        jnp.zeros((PB,), jnp.float32),
    )
    vecs, images, diagonal, offdiag = lax.fori_loop(0, PB, reflect, start_state)

    def rows_of(matrix):
        return lax.dynamic_index_in_dim(
            matrix.reshape(row_tiles, row_count, tile_size, PB), row_id, 1, keepdims=False
        ).reshape(row_width, PB)

    def cols_of(matrix):
        return lax.dynamic_index_in_dim(
            matrix.reshape(col_tiles, col_count, tile_size, PB), col_id, 1, keepdims=False
        ).reshape(col_width, PB)

    updated = (
        reduced
        - jnp.dot(rows_of(vecs), cols_of(images).T, precision=highest)
        - jnp.dot(rows_of(images), cols_of(vecs).T, precision=highest)
    )
    flat = eigvec.reshape(row_width, col_width)
    rotated = lax.psum_scatter(
        jnp.dot(psi_rows, flat, preferred_element_type=jnp.float32),
        "row",
        scatter_dimension=0,
        tiled=True,
    )
    tile_shape = (row_tiles, 1, tile_size, col_tiles, 1, tile_size)
    return (
        correlation.reshape(tile_shape),
        updated.reshape(tile_shape),
        diagonal,
        offdiag,
        rotated.astype(jnp.bfloat16).reshape(rotated.shape[0], col_tiles, 1, tile_size),
    )


def solution(mesh):
    return jax.shard_map(
        on_device,
        mesh=mesh,
        in_specs=(
            P(("row", "col"), None),
            P(("row", "col"), None),
            P(None, "row", None, None, "col", None),
        ),
        out_specs=(
            P(None, "row", None, None, "col", None),
            P(None, "row", None, None, "col", None),
            P(),
            P(),
            P("row", None, "col", None),
        ),
        check_vma=False,
    )
```

profile of v0, /device:TPU:0, one launch (start us, length us, event | category | flops | bytes accessed | tf_op | source)
XLA Modules:
  0.0 1025.6 jit_solution(13793135316026155486)
XLA Ops:
  8.4 15.9 %all_to_all.72 = bf16[1,32,4,8,128]{4,1,2,0,3:T(8,128)(2,1)S(1)} all-to-all(bf16[1,32,4,8,128]{4,1,2,0,3:T(8,128)(2,1)S(1)} %copy.46), channel_id=1, replica_groups=mesh['row'=8,'col'=4] {'row'}, dimensions={3} | all-to-all | bytes 524288 | tf_op jit(solution)/shard_map/all_to_all | solution.py:39
  25.4 12.1 %all_to_all.73 = bf16[1,32,4,8,128]{4,1,2,0,3:T(8,128)(2,1)S(1)} all-to-all(bf16[1,32,4,8,128]{4,1,2,0,3:T(8,128)(2,1)S(1)} %copy.55), channel_id=1, replica_groups=mesh['row'=8,'col'=4] {'row'}, dimensions={3} | all-to-all | bytes 524288 | tf_op jit(solution)/shard_map/all_to_all | solution.py:40
  65.2 15.7 %all-gather.13.cloned.1.call-done = bf16[8,1,128,4,1,128]{5,0,4,3,1,2:T(8,128)(2,1)} async-done(((bf16[8,1,32,4,1,128]{5,0,4,3,1,2:T(8,128)(2,1)}), bf16[8,1,128,4,1,128]{5,0,4,3,1,2:T(8,128)(2,1)}) %all-gather.13.cloned.1.call-update) | async-done | bytes 1048592 | tf_op jit(solution)/shard_map/all_gather | solution.py:44
  83.8 27.9 %all-gather.9.cloned.1.call-done = bf16[1024,8,1,128]{3,1,2,0:T(8,128)(2,1)} async-done(((bf16[128,8,1,128]{3,1,2,0:T(8,128)(2,1)}), bf16[1024,8,1,128]{3,1,2,0:T(8,128)(2,1)}) %all-gather.9.cloned.1.call-update) | async-done | bytes 2097168 | tf_op jit(solution)/shard_map/all_gather | solution.py:58
  117.6 24.2 %all-gather.7.cloned.1.call-done = bf16[1024,8,1,128]{3,1,2,0:T(8,128)(2,1)} async-done(((bf16[128,8,1,128]{3,1,2,0:T(8,128)(2,1)}), bf16[1024,8,1,128]{3,1,2,0:T(8,128)(2,1)}) %all-gather.7.cloned.1.call-update) | async-done | bytes 2097168 | tf_op jit(solution)/shard_map/all_gather | solution.py:57
  152.8 16.3 %psum.21 = f32[4,1,128,16]{2,3,0,1:T(8,128)S(1)} all-reduce(f32[4,1,128,16]{2,3,0,1:T(8,128)S(1)} %select_bitcast_fusion), channel_id=1, replica_groups=mesh['row'=8,'col'=4] {'col'}, use_global_device_ids=true, to_apply=%region_0.1 | all-reduce | flops 8192 | bytes 65536 | tf_op jit(solution)/shard_map/psum | solution.py:11
  169.1 15.8 %all_gather.29 = f32[4,8,128,16]{2,3,0,1:T(8,128)S(1)} all-gather(f32[4,1,128,16]{2,3,0,1:T(8,128)S(1)} %psum.21), channel_id=1, replica_groups=mesh['row'=8,'col'=4] {'row'}, dimensions={1}, use_global_device_ids=true | all-gather | bytes 294912 | tf_op jit(solution)/shard_map/all_gather | solution.py:67
  185.2 819.2 %while.23 = (s32[]{:T(128)}, f32[4096,16]{1,0:T(8,128)}, f32[4096,16]{1,0:T(8,128)}, f32[16]{0:T(128)S(1)}, f32[16]{0:T(128)S(1)}, /*index=5*/f32[4096,16]{0,1:T...) while((s32[]{:T(128)}, f32[4096,16]{1,0:T(8,128)}, ...), condition=%wide.region_4.5_spmd.clone.clone, body=%wide.region_1.4_spmd.clone.clone.sunk | while | flops 11387518 | bytes 10909649 | solution.py:124
  210.5 12.8 %all_gather.33 = f32[4,8,128]{2,0,1:T(4,128)S(1)} all-gather(f32[4,1,128]{2,0,1:T(4,128)S(1)} %psum.25), channel_id=1, replica_groups=mesh['row'=8,'col'=4] {'row'}, dimensions={1}, use_global_device_ids=true | all-gather | bytes 18432 | tf_op jit(solution)/shard_map/while/body/eval_jaxpr/all_gather | solution.py:77
  262.3 12.8 %all_gather.33 = f32[4,8,128]{2,0,1:T(4,128)S(1)} all-gather(f32[4,1,128]{2,0,1:T(4,128)S(1)} %psum.25), channel_id=1, replica_groups=mesh['row'=8,'col'=4] {'row'}, dimensions={1}, use_global_device_ids=true | all-gather | bytes 18432 | tf_op jit(solution)/shard_map/while/body/eval_jaxpr/all_gather | solution.py:77
  312.8 12.8 %all_gather.33 = f32[4,8,128]{2,0,1:T(4,128)S(1)} all-gather(f32[4,1,128]{2,0,1:T(4,128)S(1)} %psum.25), channel_id=1, replica_groups=mesh['row'=8,'col'=4] {'row'}, dimensions={1}, use_global_device_ids=true | all-gather | bytes 18432 | tf_op jit(solution)/shard_map/while/body/eval_jaxpr/all_gather | solution.py:77
  365.3 12.8 %all_gather.33 = f32[4,8,128]{2,0,1:T(4,128)S(1)} all-gather(f32[4,1,128]{2,0,1:T(4,128)S(1)} %psum.25), channel_id=1, replica_groups=mesh['row'=8,'col'=4] {'row'}, dimensions={1}, use_global_device_ids=true | all-gather | bytes 18432 | tf_op jit(solution)/shard_map/while/body/eval_jaxpr/all_gather | solution.py:77
  415.8 12.8 %all_gather.33 = f32[4,8,128]{2,0,1:T(4,128)S(1)} all-gather(f32[4,1,128]{2,0,1:T(4,128)S(1)} %psum.25), channel_id=1, replica_groups=mesh['row'=8,'col'=4] {'row'}, dimensions={1}, use_global_device_ids=true | all-gather | bytes 18432 | tf_op jit(solution)/shard_map/while/body/eval_jaxpr/all_gather | solution.py:77
  467.6 12.8 %all_gather.33 = f32[4,8,128]{2,0,1:T(4,128)S(1)} all-gather(f32[4,1,128]{2,0,1:T(4,128)S(1)} %psum.25), channel_id=1, replica_groups=mesh['row'=8,'col'=4] {'row'}, dimensions={1}, use_global_device_ids=true | all-gather | bytes 18432 | tf_op jit(solution)/shard_map/while/body/eval_jaxpr/all_gather | solution.py:77
  518.1 12.8 %all_gather.33 = f32[4,8,128]{2,0,1:T(4,128)S(1)} all-gather(f32[4,1,128]{2,0,1:T(4,128)S(1)} %psum.25), channel_id=1, replica_groups=mesh['row'=8,'col'=4] {'row'}, dimensions={1}, use_global_device_ids=true | all-gather | bytes 18432 | tf_op jit(solution)/shard_map/while/body/eval_jaxpr/all_gather | solution.py:77
  570.6 12.8 %all_gather.33 = f32[4,8,128]{2,0,1:T(4,128)S(1)} all-gather(f32[4,1,128]{2,0,1:T(4,128)S(1)} %psum.25), channel_id=1, replica_groups=mesh['row'=8,'col'=4] {'row'}, dimensions={1}, use_global_device_ids=true | all-gather | bytes 18432 | tf_op jit(solution)/shard_map/while/body/eval_jaxpr/all_gather | solution.py:77
  621.1 12.8 %all_gather.33 = f32[4,8,128]{2,0,1:T(4,128)S(1)} all-gather(f32[4,1,128]{2,0,1:T(4,128)S(1)} %psum.25), channel_id=1, replica_groups=mesh['row'=8,'col'=4] {'row'}, dimensions={1}, use_global_device_ids=true | all-gather | bytes 18432 | tf_op jit(solution)/shard_map/while/body/eval_jaxpr/all_gather | solution.py:77
  672.9 12.8 %all_gather.33 = f32[4,8,128]{2,0,1:T(4,128)S(1)} all-gather(f32[4,1,128]{2,0,1:T(4,128)S(1)} %psum.25), channel_id=1, replica_groups=mesh['row'=8,'col'=4] {'row'}, dimensions={1}, use_global_device_ids=true | all-gather | bytes 18432 | tf_op jit(solution)/shard_map/while/body/eval_jaxpr/all_gather | solution.py:77
  723.4 12.8 %all_gather.33 = f32[4,8,128]{2,0,1:T(4,128)S(1)} all-gather(f32[4,1,128]{2,0,1:T(4,128)S(1)} %psum.25), channel_id=1, replica_groups=mesh['row'=8,'col'=4] {'row'}, dimensions={1}, use_global_device_ids=true | all-gather | bytes 18432 | tf_op jit(solution)/shard_map/while/body/eval_jaxpr/all_gather | solution.py:77
  776.0 12.8 %all_gather.33 = f32[4,8,128]{2,0,1:T(4,128)S(1)} all-gather(f32[4,1,128]{2,0,1:T(4,128)S(1)} %psum.25), channel_id=1, replica_groups=mesh['row'=8,'col'=4] {'row'}, dimensions={1}, use_global_device_ids=true | all-gather | bytes 18432 | tf_op jit(solution)/shard_map/while/body/eval_jaxpr/all_gather | solution.py:77
  826.5 12.8 %all_gather.33 = f32[4,8,128]{2,0,1:T(4,128)S(1)} all-gather(f32[4,1,128]{2,0,1:T(4,128)S(1)} %psum.25), channel_id=1, replica_groups=mesh['row'=8,'col'=4] {'row'}, dimensions={1}, use_global_device_ids=true | all-gather | bytes 18432 | tf_op jit(solution)/shard_map/while/body/eval_jaxpr/all_gather | solution.py:77
  878.3 12.8 %all_gather.33 = f32[4,8,128]{2,0,1:T(4,128)S(1)} all-gather(f32[4,1,128]{2,0,1:T(4,128)S(1)} %psum.25), channel_id=1, replica_groups=mesh['row'=8,'col'=4] {'row'}, dimensions={1}, use_global_device_ids=true | all-gather | bytes 18432 | tf_op jit(solution)/shard_map/while/body/eval_jaxpr/all_gather | solution.py:77
  928.8 12.8 %all_gather.33 = f32[4,8,128]{2,0,1:T(4,128)S(1)} all-gather(f32[4,1,128]{2,0,1:T(4,128)S(1)} %psum.25), channel_id=1, replica_groups=mesh['row'=8,'col'=4] {'row'}, dimensions={1}, use_global_device_ids=true | all-gather | bytes 18432 | tf_op jit(solution)/shard_map/while/body/eval_jaxpr/all_gather | solution.py:77
  981.3 12.8 %all_gather.33 = f32[4,8,128]{2,0,1:T(4,128)S(1)} all-gather(f32[4,1,128]{2,0,1:T(4,128)S(1)} %psum.25), channel_id=1, replica_groups=mesh['row'=8,'col'=4] {'row'}, dimensions={1}, use_global_device_ids=true | all-gather | bytes 18432 | tf_op jit(solution)/shard_map/while/body/eval_jaxpr/all_gather | solution.py:77
  (402 shorter events, 602.6 us)
Async XLA Ops:
  7.2 18.0 %copy-start.4 = (bf16[32,4096]{1,0:T(8,128)(2,1)S(1)}, bf16[32,4096]{1,0:T(8,128)(2,1)}, u32[]{:S(2)}) copy-start(bf16[32,4096]{1,0:T(8,128)(2,1)} %param.6) | copy-start | bytes 786436
  7.2 52.5 %all-gather.11.cloned.1.call-start = ((), (), s32[]{:S(2)}) async-start(), calls=%async_computation.8 | async-start | bytes 1310720 | tf_op jit(solution)/shard_map/all_gather | solution.py:43
  25.1 55.8 %all-gather.13.cloned.1.call-start = ((), (), s32[]{:S(2)}) async-start(), calls=%async_computation.9 | async-start | bytes 1310720 | tf_op jit(solution)/shard_map/all_gather | solution.py:44
  25.2 25.4 %copy-start.5 = (bf16[32,4096]{1,0:T(8,128)(2,1)S(1)}, bf16[32,4096]{1,0:T(8,128)(2,1)}, u32[]{:S(2)}) copy-start(bf16[32,4096]{1,0:T(8,128)(2,1)} %param.5) | copy-start | bytes 786436
  38.4 73.3 %all-gather.9.cloned.1.call-start = ((), (), s32[]{:S(2)}) async-start(), calls=%async_computation.6 | async-start | bytes 2359296 | tf_op jit(solution)/shard_map/all_gather | solution.py:58
  50.5 11.5 %copy-start.8 = (bf16[4,1,128,8,1,128]{5,3,4,2,1,0:T(8,128)(2,1)S(1)}, bf16[4,1,128,8,1,128]{5,3,4,2,1,0:T(8,128)(2,1)}, u32[]{:S(2)}) copy-start(bf16[4,1,128,8,1,128]{5,3,4,2,1,0:T(8,128)(2,1)} %param.7) | copy-start | bytes 3145732
  50.5 91.2 %all-gather.7.cloned.1.call-start = ((), (), s32[]{:S(2)}) async-start(), calls=%async_computation.5 | async-start | bytes 2359296 | tf_op jit(solution)/shard_map/all_gather | solution.py:57
  59.6 957.6 %reduce-scatter.2.cloned.1.call-start = ((), (), s32[]{:S(2)}) async-start(), calls=%async_computation.7 | async-start | bytes 4718592 | tf_op jit(solution)/shard_map/reduce_scatter | solution.py:142
  145.0 4.0 copy-start.3
  185.5 3.6 copy-start
  236.1 3.6 copy-start
  287.9 3.6 copy-start
  338.4 3.6 copy-start
  390.9 3.6 copy-start
  441.4 3.6 copy-start
  493.2 3.6 copy-start
  596.2 3.6 copy-start
  646.7 3.6 copy-start
  698.5 3.6 copy-start
  749.0 3.6 copy-start
  801.6 3.6 copy-start
  852.1 3.6 copy-start
  903.9 3.6 copy-start
  954.4 3.6 copy-start
  (5 other events, 14.7 us)
Sparse Core Ops, SparseCore 0:
  25.2 27.5 all-gather.10
  55.3 25.5 all-gather.12
  82.5 29.1 all-gather.8
  113.2 28.5 all-gather.6
  143.9 51.4 reduce-scatter.1
where the time goes:
time: 1030 us
  blocking collectives  423 us (41%)
  matrix products  275 us (27%)
  other arithmetic  131 us (13%)
  loops' own time  77 us (7%)
  waiting for transfers between devices  67.9 us (7%)
  local copies, waits for them, and re-layouts  36.9 us (4%)
  between operations  14.1 us (1%)
    all_gather x16, blocking collectives, product(): lax.all_gather(summed.reshape(row_tiles, 1, tile_size), 'row', axis=1, ti...  204 us
    psum x16, blocking collectives, product(): summed = lax.psum(partial_sum, 'col')  139 us
    another operation x1, loops' own time, on_device(): vecs, images, diagonal, offdiag = lax.fori_loop(0, PB, reflect, start_state)  77 us
    select_n x16, other arithmetic, reflect(): images = jnp.where(pick[None, :], image[:, None], images)  61.2 us
    while x16, matrix products  56.5 us
    dot_general x16, matrix products, reflect(): jnp.dot(images, jnp.dot(vector, vecs, precision=highest), precision=highest)  54 us
    dot_general x16, matrix products, reflect(): jnp.dot(vector, images, precision=highest)  43.2 us
    while x16, other arithmetic  37.8 us
  transfers between devices with their start and end apart: 5, of which 3 were waited for; matrix products, arithmetic and copies ran while one was open for 43% of the time, Pallas kernels for 0%

commit v1 on v0

--- a/solution.py
+++ b/solution.py
@@ -73,7 +73,9 @@
             vector.reshape(col_tiles, col_count, tile_size), col_id, 1, keepdims=False
         )
         partial_sum = jnp.einsum("atbs,bs->at", blocks, local_vec, precision=highest)
-        summed = lax.psum(partial_sum, "col")
+        summed = partial_sum
+        for hop in (1, 2):
+            summed = summed + lax.ppermute(summed, "col", [(dev, dev ^ hop) for dev in range(4)])
         result = lax.all_gather(
             summed.reshape(row_tiles, 1, tile_size), "row", axis=1, tiled=True
         ).reshape(bands)

time: 1030 us -> 896 us (0.87)
  blocking collectives: 423 us -> 285 us
  matrix products: 275 us -> 222 us
  waiting for transfers between devices: 67.9 us -> 102 us
  starting transfers between devices: 0.21 us -> 30.4 us
    psum x16 -> x0, blocking collectives: 139 us -> none  [product(): summed = lax.psum(partial_sum, 'col')]
    ppermute x0 -> x32, waiting for transfers between devices: none -> 34 us  [product(): lax.ppermute(summed, 'col', [(dev, dev ^ hop) for dev in range(4)])]
    ppermute x0 -> x32, starting transfers between devices: none -> 30.2 us  [product(): lax.ppermute(summed, 'col', [(dev, dev ^ hop) for dev in range(4)])]
    dot_general x16, matrix products: 43.2 us -> 17.8 us  [reflect(): jnp.dot(vector, images, precision=highest)]
    dot_general x16, matrix products: 54 us -> 28.8 us  [reflect(): jnp.dot(images, jnp.dot(vector, vecs, precision=highest), precision=highest)]
  transfers between devices with their start and end apart: 5 -> 37, of which waited for: 3 -> 19; matrix products, arithmetic and copies ran while one was open for 43% -> 43% of each run, Pallas kernels for 0% -> 0%
where the time goes in v1:
time: 896 us; the launch traced here: 894 us
  blocking collectives  285 us (32%)
  matrix products  222 us (25%)
  other arithmetic  132 us (15%)
  waiting for transfers between devices  102 us (11%)
  loops' own time  72.9 us (8%)
  local copies, waits for them, and re-layouts  36.1 us (4%)
  starting transfers between devices  30.4 us (3%)
  between operations  14.1 us (2%)
    all_gather x16, blocking collectives, product(): lax.all_gather(summed.reshape(row_tiles, 1, tile_size), 'row', axis=1, ti...  204 us
    another operation x1, loops' own time, on_device(): vecs, images, diagonal, offdiag = lax.fori_loop(0, PB, reflect, start_state)  72.9 us
    select_n x16, other arithmetic, reflect(): images = jnp.where(pick[None, :], image[:, None], images)  61.9 us
    while x16, matrix products  58.6 us
    while x16, other arithmetic  37.7 us
    ppermute x32, waiting for transfers between devices, product(): lax.ppermute(summed, 'col', [(dev, dev ^ hop) for dev in range(4)])  34 us
    ppermute x32, starting transfers between devices, product(): lax.ppermute(summed, 'col', [(dev, dev ^ hop) for dev in range(4)])  30.2 us
    dot_general x16, matrix products, reflect(): jnp.dot(vecs, jnp.dot(vector, images, precision=highest), precision=highest)  29 us
  transfers between devices with their start and end apart: 37, of which 19 were waited for; matrix products, arithmetic and copies ran while one was open for 43% of the time, Pallas kernels for 0%

profile of v1, /device:TPU:0, one launch (start us, length us, event | category | flops | bytes accessed | tf_op | source)
XLA Modules:
  0.0 894.0 jit_solution(15888798769072788288)
XLA Ops:
  8.4 15.9 %all_to_all.72 = bf16[1,32,4,8,128]{4,1,2,0,3:T(8,128)(2,1)S(1)} all-to-all(bf16[1,32,4,8,128]{4,1,2,0,3:T(8,128)(2,1)S(1)} %copy.44), channel_id=1, replica_groups=mesh['row'=8,'col'=4] {'row'}, dimensions={3} | all-to-all | bytes 524288 | tf_op jit(solution)/shard_map/all_to_all | solution.py:39
  25.4 12.1 %all_to_all.73 = bf16[1,32,4,8,128]{4,1,2,0,3:T(8,128)(2,1)S(1)} all-to-all(bf16[1,32,4,8,128]{4,1,2,0,3:T(8,128)(2,1)S(1)} %copy.53), channel_id=1, replica_groups=mesh['row'=8,'col'=4] {'row'}, dimensions={3} | all-to-all | bytes 524288 | tf_op jit(solution)/shard_map/all_to_all | solution.py:40
  65.2 15.7 %all-gather.17.cloned.1.call-done = bf16[8,1,128,4,1,128]{5,0,4,3,1,2:T(8,128)(2,1)} async-done(((bf16[8,1,32,4,1,128]{5,0,4,3,1,2:T(8,128)(2,1)}), bf16[8,1,128,4,1,128]{5,0,4,3,1,2:T(8,128)(2,1)}) %all-gather.17.cloned.1.call-update) | async-done | bytes 1048592 | tf_op jit(solution)/shard_map/all_gather | solution.py:44
  83.8 27.9 %all-gather.13.cloned.1.call-done = bf16[1024,8,1,128]{3,1,2,0:T(8,128)(2,1)} async-done(((bf16[128,8,1,128]{3,1,2,0:T(8,128)(2,1)}), bf16[1024,8,1,128]{3,1,2,0:T(8,128)(2,1)}) %all-gather.13.cloned.1.call-update) | async-done | bytes 2097168 | tf_op jit(solution)/shard_map/all_gather | solution.py:58
  117.6 24.2 %all-gather.11.cloned.1.call-done = bf16[1024,8,1,128]{3,1,2,0:T(8,128)(2,1)} async-done(((bf16[128,8,1,128]{3,1,2,0:T(8,128)(2,1)}), bf16[1024,8,1,128]{3,1,2,0:T(8,128)(2,1)}) %all-gather.11.cloned.1.call-update) | async-done | bytes 2097168 | tf_op jit(solution)/shard_map/all_gather | solution.py:57
  153.2 16.3 %psum.7 = f32[4,1,128,16]{2,3,0,1:T(8,128)S(1)} all-reduce(f32[4,1,128,16]{2,3,0,1:T(8,128)S(1)} %select_bitcast_fusion), channel_id=1, replica_groups=mesh['row'=8,'col'=4] {'col'}, use_global_device_ids=true, to_apply=%region_0.1 | all-reduce | flops 8192 | bytes 65536 | tf_op jit(solution)/shard_map/psum | solution.py:11
  169.5 15.8 %all_gather.29 = f32[4,8,128,16]{2,3,0,1:T(8,128)S(1)} all-gather(f32[4,1,128,16]{2,3,0,1:T(8,128)S(1)} %psum.7), channel_id=1, replica_groups=mesh['row'=8,'col'=4] {'row'}, dimensions={1}, use_global_device_ids=true | all-gather | bytes 294912 | tf_op jit(solution)/shard_map/all_gather | solution.py:67
  185.5 691.9 %while.23 = (s32[]{:T(128)}, f32[4096,16]{1,0:T(8,128)}, f32[4096,16]{1,0:T(8,128)}, f32[16]{0:T(128)S(1)}, f32[16]{0:T(128)S(1)}, /*index=5*/f32[4096,16]{0,1:T...) while((s32[]{:T(128)}, f32[4096,16]{1,0:T(8,128)}, ...), condition=%wide.region_3.4_spmd.clone.clone, body=%wide.region_1.3_spmd.clone.clone.sunk | while | flops 11388030 | bytes 11982909 | solution.py:126
  207.8 12.8 %all-gather.5 = f32[4,1024]{1,0:T(4,128)S(1)} all-gather(f32[4,128]{1,0:T(4,128)S(1)} %add.145), channel_id=4, replica_groups=mesh['row'=8,'col'=4] {'row'}, dimensions={1}, use_global_device_ids=true | all-gather | bytes 18432 | tf_op jit(solution)/shard_map/while/body/eval_jaxpr/all_gather | solution.py:79
  252.2 12.8 %all-gather.5 = f32[4,1024]{1,0:T(4,128)S(1)} all-gather(f32[4,128]{1,0:T(4,128)S(1)} %add.145), channel_id=4, replica_groups=mesh['row'=8,'col'=4] {'row'}, dimensions={1}, use_global_device_ids=true | all-gather | bytes 18432 | tf_op jit(solution)/shard_map/while/body/eval_jaxpr/all_gather | solution.py:79
  294.6 12.8 %all-gather.5 = f32[4,1024]{1,0:T(4,128)S(1)} all-gather(f32[4,128]{1,0:T(4,128)S(1)} %add.145), channel_id=4, replica_groups=mesh['row'=8,'col'=4] {'row'}, dimensions={1}, use_global_device_ids=true | all-gather | bytes 18432 | tf_op jit(solution)/shard_map/while/body/eval_jaxpr/all_gather | solution.py:79
  339.0 12.8 %all-gather.5 = f32[4,1024]{1,0:T(4,128)S(1)} all-gather(f32[4,128]{1,0:T(4,128)S(1)} %add.145), channel_id=4, replica_groups=mesh['row'=8,'col'=4] {'row'}, dimensions={1}, use_global_device_ids=true | all-gather | bytes 18432 | tf_op jit(solution)/shard_map/while/body/eval_jaxpr/all_gather | solution.py:79
  381.3 12.8 %all-gather.5 = f32[4,1024]{1,0:T(4,128)S(1)} all-gather(f32[4,128]{1,0:T(4,128)S(1)} %add.145), channel_id=4, replica_groups=mesh['row'=8,'col'=4] {'row'}, dimensions={1}, use_global_device_ids=true | all-gather | bytes 18432 | tf_op jit(solution)/shard_map/while/body/eval_jaxpr/all_gather | solution.py:79
  425.7 12.8 %all-gather.5 = f32[4,1024]{1,0:T(4,128)S(1)} all-gather(f32[4,128]{1,0:T(4,128)S(1)} %add.145), channel_id=4, replica_groups=mesh['row'=8,'col'=4] {'row'}, dimensions={1}, use_global_device_ids=true | all-gather | bytes 18432 | tf_op jit(solution)/shard_map/while/body/eval_jaxpr/all_gather | solution.py:79
  468.1 12.8 %all-gather.5 = f32[4,1024]{1,0:T(4,128)S(1)} all-gather(f32[4,128]{1,0:T(4,128)S(1)} %add.145), channel_id=4, replica_groups=mesh['row'=8,'col'=4] {'row'}, dimensions={1}, use_global_device_ids=true | all-gather | bytes 18432 | tf_op jit(solution)/shard_map/while/body/eval_jaxpr/all_gather | solution.py:79
  512.5 12.8 %all-gather.5 = f32[4,1024]{1,0:T(4,128)S(1)} all-gather(f32[4,128]{1,0:T(4,128)S(1)} %add.145), channel_id=4, replica_groups=mesh['row'=8,'col'=4] {'row'}, dimensions={1}, use_global_device_ids=true | all-gather | bytes 18432 | tf_op jit(solution)/shard_map/while/body/eval_jaxpr/all_gather | solution.py:79
  554.9 12.8 %all-gather.5 = f32[4,1024]{1,0:T(4,128)S(1)} all-gather(f32[4,128]{1,0:T(4,128)S(1)} %add.145), channel_id=4, replica_groups=mesh['row'=8,'col'=4] {'row'}, dimensions={1}, use_global_device_ids=true | all-gather | bytes 18432 | tf_op jit(solution)/shard_map/while/body/eval_jaxpr/all_gather | solution.py:79
  599.3 12.8 %all-gather.5 = f32[4,1024]{1,0:T(4,128)S(1)} all-gather(f32[4,128]{1,0:T(4,128)S(1)} %add.145), channel_id=4, replica_groups=mesh['row'=8,'col'=4] {'row'}, dimensions={1}, use_global_device_ids=true | all-gather | bytes 18432 | tf_op jit(solution)/shard_map/while/body/eval_jaxpr/all_gather | solution.py:79
  641.6 12.8 %all-gather.5 = f32[4,1024]{1,0:T(4,128)S(1)} all-gather(f32[4,128]{1,0:T(4,128)S(1)} %add.145), channel_id=4, replica_groups=mesh['row'=8,'col'=4] {'row'}, dimensions={1}, use_global_device_ids=true | all-gather | bytes 18432 | tf_op jit(solution)/shard_map/while/body/eval_jaxpr/all_gather | solution.py:79
  686.0 12.8 %all-gather.5 = f32[4,1024]{1,0:T(4,128)S(1)} all-gather(f32[4,128]{1,0:T(4,128)S(1)} %add.145), channel_id=4, replica_groups=mesh['row'=8,'col'=4] {'row'}, dimensions={1}, use_global_device_ids=true | all-gather | bytes 18432 | tf_op jit(solution)/shard_map/while/body/eval_jaxpr/all_gather | solution.py:79
  728.4 12.8 %all-gather.5 = f32[4,1024]{1,0:T(4,128)S(1)} all-gather(f32[4,128]{1,0:T(4,128)S(1)} %add.145), channel_id=4, replica_groups=mesh['row'=8,'col'=4] {'row'}, dimensions={1}, use_global_device_ids=true | all-gather | bytes 18432 | tf_op jit(solution)/shard_map/while/body/eval_jaxpr/all_gather | solution.py:79
  772.8 12.8 %all-gather.5 = f32[4,1024]{1,0:T(4,128)S(1)} all-gather(f32[4,128]{1,0:T(4,128)S(1)} %add.145), channel_id=4, replica_groups=mesh['row'=8,'col'=4] {'row'}, dimensions={1}, use_global_device_ids=true | all-gather | bytes 18432 | tf_op jit(solution)/shard_map/while/body/eval_jaxpr/all_gather | solution.py:79
  815.1 12.8 %all-gather.5 = f32[4,1024]{1,0:T(4,128)S(1)} all-gather(f32[4,128]{1,0:T(4,128)S(1)} %add.145), channel_id=4, replica_groups=mesh['row'=8,'col'=4] {'row'}, dimensions={1}, use_global_device_ids=true | all-gather | bytes 18432 | tf_op jit(solution)/shard_map/while/body/eval_jaxpr/all_gather | solution.py:79
  859.5 12.8 %all-gather.5 = f32[4,1024]{1,0:T(4,128)S(1)} all-gather(f32[4,128]{1,0:T(4,128)S(1)} %add.145), channel_id=4, replica_groups=mesh['row'=8,'col'=4] {'row'}, dimensions={1}, use_global_device_ids=true | all-gather | bytes 18432 | tf_op jit(solution)/shard_map/while/body/eval_jaxpr/all_gather | solution.py:79
  (518 shorter events, 475.1 us)
Async XLA Ops:
  7.2 52.6 %all-gather.15.cloned.1.call-start = ((), (), s32[]{:S(2)}) async-start(), calls=%async_computation.8 | async-start | bytes 1310720 | tf_op jit(solution)/shard_map/all_gather | solution.py:43
  25.1 55.8 %all-gather.17.cloned.1.call-start = ((), (), s32[]{:S(2)}) async-start(), calls=%async_computation.9 | async-start | bytes 1310720 | tf_op jit(solution)/shard_map/all_gather | solution.py:44
  38.4 73.3 %all-gather.13.cloned.1.call-start = ((), (), s32[]{:S(2)}) async-start(), calls=%async_computation.6 | async-start | bytes 2359296 | tf_op jit(solution)/shard_map/all_gather | solution.py:58
  50.5 91.2 %all-gather.11.cloned.1.call-start = ((), (), s32[]{:S(2)}) async-start(), calls=%async_computation.5 | async-start | bytes 2359296 | tf_op jit(solution)/shard_map/all_gather | solution.py:57
  59.6 826.0 %reduce-scatter.2.cloned.1.call-start = ((), (), s32[]{:S(2)}) async-start(), calls=%async_computation.7 | async-start | bytes 4718592 | tf_op jit(solution)/shard_map/reduce_scatter | solution.py:144
  197.6 6.6 collective-permute-start
  204.2 3.7 collective-permute-start.1
  239.9 8.6 collective-permute-start
  284.3 6.6 collective-permute-start
  326.7 8.6 collective-permute-start
  371.1 6.6 collective-permute-start
  413.5 8.6 collective-permute-start
  457.9 6.6 collective-permute-start
  500.2 8.6 collective-permute-start
  544.6 6.6 collective-permute-start
  587.0 8.6 collective-permute-start
  631.4 6.6 collective-permute-start
  673.7 8.6 collective-permute-start
  682.4 3.7 collective-permute-start.1
  718.1 6.6 collective-permute-start
  724.7 3.7 collective-permute-start.1
  760.5 8.6 collective-permute-start
  804.9 6.6 collective-permute-start
  847.3 8.6 collective-permute-start
  (55 other events, 226.0 us)
Sparse Core Ops, SparseCore 0:
  25.2 27.5 all-gather.14
  55.3 25.5 all-gather.16
  82.5 29.1 all-gather.12
  113.2 28.5 all-gather.10
  143.9 51.4 reduce-scatter.1
